TPU v7x, 32 devices: a whole 2x2x4 slice. The times are simulated.
32 devices in a mesh: dp: 4 (over y, x), vocab: 8 (over z, core).
Axes of the slice: x: 2, y: 2, z: 4, core: 2. Of those that a mesh axis runs over, the one named last changes fastest.
Arguments:
- hidden: bfloat16 [256, 3072], P(('dp', 'vocab')), parts along dimension 0, may hold values from -60 to 60
- weight: bfloat16 [3072, 8192], P(None, 'vocab'), may hold values from -0.32421875 to 0.32421875
- targets: int32 [256], P('dp'), parts along dimension 0, may hold values from 0 to 8191
Outputs:
- loss: float32 [4], P('dp'), parts along dimension 0
- d_hidden: bfloat16 [256, 3072], P(('dp', 'vocab')), parts along dimension 0
- d_weight: bfloat16 [12288, 8192], P('dp', 'vocab'), parts along dimension 0
There are 4 independent parts, one for each index of `dp`. A program takes and returns all parts, laid end to end along the dimension named above; an argument that names none is the same for every part. Nothing has to cross between parts.
All inputs are finite; a program needn't handle non-finite values.
Results may differ from a plain program's by a relative error of at most 0.0035.
Values may be sent and summed in bfloat16 or wider, within the bound.
A program may use at most 64 MiB of HBM per device.

v0:
```python
import jax
import jax.numpy as jnp
from jax import lax
from jax.sharding import PartitionSpec as P


def joined(value, axis, combine):
    everything = jax.tree.map(lambda part: lax.all_gather(part, axis), value)
    initial = jax.tree.map(lambda part: part[0], everything)

    def hop(k, so_far):
        return combine(so_far, jax.tree.map(lambda part: part[k], everything))

    return lax.fori_loop(1, lax.axis_size(axis), hop, initial)


def combine_stats(first, second):
    top = jnp.maximum(first[0], second[0])
    total = first[1] * jnp.exp(first[0] - top) + second[1] * jnp.exp(second[0] - top)
    return (top, total, first[2] + second[2])


def body(hidden, weight, targets):
    gathered = lax.all_gather(hidden, "vocab", axis=0, tiled=True)
    logits = jnp.dot(gathered, weight, preferred_element_type=jnp.float32)
    width = weight.shape[1]
    offset = lax.axis_index("vocab") * width
    columns = offset + lax.broadcasted_iota(jnp.int32, (1, width), 1)
    hits = columns == targets[:, None]
    picked_local = jnp.sum(jnp.where(hits, logits, jnp.zeros_like(logits)), axis=1)
    local_top = jnp.max(logits, axis=1)
    local_total = jnp.sum(jnp.exp(logits - local_top[:, None]), axis=1)
    top, total, picked = joined((local_top, local_total, picked_local), "vocab", combine_stats)
    loss = jnp.mean(top + jnp.log(total) - picked).reshape(1)
    grad_logits = (
        jnp.exp(logits - top[:, None]) / total[:, None] - hits.astype(jnp.float32)
    ).astype(jnp.bfloat16)
    d_weight = lax.dot_general(
        gathered, grad_logits, (((0,), (0,)), ((), ())), preferred_element_type=jnp.float32
    ).astype(jnp.bfloat16)
    own_rows = hidden.shape[0]
    partial_value = lax.dot_general(
        grad_logits, weight, (((1,), (1,)), ((), ())), preferred_element_type=jnp.float32
    )
    everything = lax.psum(partial_value, "vocab")
    summed = lax.dynamic_slice_in_dim(everything, lax.axis_index("vocab") * own_rows, own_rows, 0)
    return (loss, summed.astype(jnp.bfloat16), d_weight)


def solution(mesh):
    placed = (P(("dp", "vocab"), None), P(None, "vocab"), P("dp"))
    return jax.shard_map(
        body,
        mesh=mesh,
        in_specs=placed,
        out_specs=(P("dp"), P(("dp", "vocab"), None), P("dp", "vocab")),
        check_vma=False,
    )
```

profile of v0, /device:TPU:0, one launch (start us, length us, event | category | flops | bytes accessed | tf_op | source)
XLA Modules:
  0.0 96.6 jit_solution(8625070616558614490)
XLA Ops:
  0.6 0.0 copy-start
  0.6 1.2 %dynamic-slice = u32[1]{0:T(128)} dynamic-slice(u32[32]{0:T(128)} %constant.59, u32[]{:T(128)S(6)} %add.78), dynamic_slice_sizes={1} | dynamic-slice | bytes 12
  2.6 16.4 %all_gather.21 = bf16[64,3072]{1,0:T(8,128)(2,1)S(1)} all-gather(bf16[8,3072]{1,0:T(8,128)(2,1)} %param.5), channel_id=1, replica_groups=mesh['dp'=4,'vocab'=8] {'vocab'}, dimensions={0}, use_global_device_ids=true | all-gather | bytes 442368 | tf_op jit(solution)/shard_map/all_gather | solution.py:24
  19.0 4.1 %fusion.14 = (f32[64]{0:T(128)S(1)}, f32[64,1024]{1,0:T(8,128)S(1)}) fusion(bf16[64,3072]{1,0:T(8,128)(2,1)S(1)} %all_gather.21, bf16[3072,1024]{1,0:T(8,128)(2,1)} %param.6), kind=kOutput, calls=%fused_computation.21 | convolution fusion | flops 402718656 | bytes 6947072 | tf_op jit(solution)/shard_map/dot_general | solution.py:25
  23.1 0.2 dynamic-update-slice
  23.4 0.0 copy-done
  23.4 0.2 fusion.7
  23.6 0.2 dynamic-update-slice.2
  23.8 0.2 dynamic-update-slice.1
  24.0 17.2 %all-reduce.3 = (f32[512]{0:T(512)S(1)}, f32[512]{0:T(512)S(1)}, f32[512]{0:T(512)S(1)}) all-reduce(f32[512]{0:T(512)S(1)} %dynamic-update-slice, f32[512]{0:T(512)S(1)} %dynamic-update-slice.1, f32[512]{0:T(512)S(1)} %dynamic-update-slice.2), channel_id=2, replica_groups=mesh['dp'=4,'vocab'=8] {'vocab'}, use_global_device_ids=true, to_apply=%add | all-reduce | flops 1536 | bytes 12288
  41.2 0.1 reshape.21
  41.3 0.1 reshape.20
  41.4 0.1 reshape.19
  41.5 0.3 while.19
  41.8 0.6 subtract_reduce_fusion
  43.0 4.8 %fusion.11 = f32[64,3072]{1,0:T(8,128)S(1)} fusion(bf16[3072,1024]{1,0:T(8,128)(2,1)} %param.6, f32[64,1024]{1,0:T(8,128)S(1)} %get-tuple-element.210, f32[64]{0:T(128)S(1)} %get-tuple-element.182, f32[64]{0:T(128)S(1)} %get-tuple-element.181, s32[1024]{0:T(1024)S(1)} %iota_add_fusion, s32[64]{0:T(128)S(1)} %copy-done), kind=kOutput, calls=%fused_computation.20 | convolution fusion | flops 403046400 | bytes 7344896 | tf_op jit(solution)/shard_map/dot_general | solution.py:42
  47.9 33.8 %all-reduce.5 = bf16[64,3072]{1,0:T(8,128)(2,1)S(1)} all-reduce(f32[64,3072]{1,0:T(8,128)S(1)} %fusion.11), channel_id=1, replica_groups=mesh['dp'=4,'vocab'=8] {'vocab'}, use_global_device_ids=true, to_apply=%region_6.7 | all-reduce | flops 196608 | bytes 1179648 | tf_op jit(solution)/shard_map/psum | solution.py:45
  81.7 0.6 dynamic-slice_convert_fusion
  82.3 4.6 %convert_bitcast_fusion = bf16[3072,1024]{0,1:T(8,128)(2,1)} fusion(bf16[64,3072]{1,0:T(8,128)(2,1)S(1)} %all_gather.21, f32[64,1024]{1,0:T(8,128)S(1)} %get-tuple-element.210, f32[64]{0:T(128)S(1)} %get-tuple-element.182, f32[64]{0:T(128)S(1)} %get-tuple-element.181, s32[1024]{0:T(1024)S(1)} %iota_add_fusion, s32[64]{0:T(128)S(1)} %copy-done), kind=kOutput, calls=%fused_computation.10 | convolution fusion | flops 406192128 | bytes 6951680 | tf_op jit(solution)/shard_map/dot_general | solution.py:38
  86.9 8.6 %copy.6 = bf16[3072,1024]{1,0:T(8,128)(2,1)} copy(bf16[3072,1024]{0,1:T(8,128)(2,1)} %convert_bitcast_fusion) | data formatting | bytes 12582912
  (14 shorter events, 0.2 us)
Async XLA Ops:
  0.6 22.7 %copy-start = (s32[64]{0:T(128)S(1)}, s32[64]{0:T(128)}, u32[]{:S(2)}) copy-start(s32[64]{0:T(128)} %param.7) | copy-start | bytes 772
where the time goes:
time: 97.1 us; the launch traced here: 96.6 us
  blocking collectives  67.4 us (69%)
  matrix products  13.5 us (14%)
  local copies, waits for them, and re-layouts  11.4 us (12%)
  between operations  3.16 us (3%)
  other arithmetic  1.03 us (1%)
    psum x1, blocking collectives, body(): everything = lax.psum(partial_value, 'vocab')  33.8 us
    unnamed x1, blocking collectives  17.2 us
    all_gather x1, blocking collectives, body(): gathered = lax.all_gather(hidden, 'vocab', axis=0, tiled=True)  16.4 us
    unnamed x10, local copies, waits for them, and re-layouts  10.5 us
    dot_general x1, matrix products, body(): lax.dot_general(grad_logits, weight, (((1,), (1,)), ((), ())), preferred_...  4.85 us
    dot_general x1, matrix products, body(): lax.dot_general(gathered, grad_logits, (((0,), (0,)), ((), ())), preferre...  4.58 us
    dot_general x1, matrix products, body(): logits = jnp.dot(gathered, weight, preferred_element_type=jnp.float32)  4.09 us

commit v1 on v0

v1 whole, which is shorter than its diff:
```python
import functools

import jax
import jax.numpy as jnp
from jax import lax
from jax.experimental import pallas as pl
from jax.experimental.pallas import tpu as pltpu
from jax.sharding import PartitionSpec as P

MESH = pl.DeviceIdType.MESH
F32 = jnp.float32
BF16 = jnp.bfloat16


def split(length, most, unit):
    for parts in range(most, 0, -1):
        if length % (parts * unit) == 0:
            return parts
    return 1


def remote(src, dst, send, recv, device):
    return pltpu.make_async_remote_copy(
        src_ref=src, dst_ref=dst, send_sem=send, recv_sem=recv, device_id={"vocab": device}, device_id_type=MESH
    )


def loss_kernel(
    n, h_ref, w_hbm, t_ref, hid_ref, g_ref, dh_ref, loss_ref,
    w_v, slots, e_v, stats, part, xbuf, outb, rbuf,
    w_sem, ag_send, fw_send, ag_recv, st_send, st_recv, x_send, x_recv, rs_send, rs_recv,
):
    me = lax.axis_index("vocab")
    chips = n // 2
    chip, core = me // 2, me % 2
    partner = chip * 2 + (1 - core)
    rows, depth = h_ref.shape
    tokens, width = e_v.shape
    pieces, span = slots.shape[0], slots.shape[3]
    parts, wide = part.shape[0], part.shape[4]

    def other(k):
        return lax.rem(chip + k, chips)

    loads = [
        pltpu.make_async_copy(w_hbm.at[pl.ds(a * span, span), :], w_v.at[pl.ds(a * span, span), :], w_sem.at[a])
        for a in range(pieces)
    ]
    for load in loads:
        load.start()

    barrier = pltpu.get_barrier_semaphore()
    for k in range(1, n):
        pl.semaphore_signal(barrier, inc=1, device_id={"vocab": lax.rem(me + k, n)}, device_id_type=MESH)
    for a in range(pieces):
        slots[a, me] = h_ref[:, a * span:(a + 1) * span]
    pl.semaphore_wait(barrier, n - 1)

    sends = []
    for a in range(pieces):
        own = h_ref.at[:, pl.ds(a * span, span)]
        for k in range(chips):
            target = partner if k == 0 else other(k) * 2 + core
            copy = remote(own, slots.at[a, me], ag_send.at[a, k], ag_recv.at[a, me], target)
            copy.start()
            sends.append(copy)

    for a in range(pieces):
        for k in range(1, chips):
            source = other(k) * 2 + core
            copy = remote(slots.at[a, source], slots.at[a, source], fw_send.at[a, k], ag_recv.at[a, source], partner)
            copy.wait_recv()
            copy.start()
            sends.append(copy)
        for k in range(chips):
            source = other(k) * 2 + (1 - core)
            remote(slots.at[a, source], slots.at[a, source], fw_send.at[a, k], ag_recv.at[a, source], partner).wait_recv()
        for z in range(chips):
            both = jnp.concatenate([slots[a, 2 * z].astype(F32), slots[a, 2 * z + 1].astype(F32)], axis=0)
            hid_ref[2 * rows * z:2 * rows * (z + 1), a * span:(a + 1) * span] = both.astype(BF16)
        loads[a].wait()
        term = jnp.dot(
            hid_ref[:, a * span:(a + 1) * span], w_v[a * span:(a + 1) * span, :], preferred_element_type=F32
        )
        if a == 0:
            e_v[...] = term
        else:
            e_v[...] += term

    logits = e_v[...]
    target = jnp.transpose(jnp.broadcast_to(t_ref[...].astype(F32), (128, tokens)))[:, 0:1]
    columns = (me * width + lax.broadcasted_iota(jnp.int32, (tokens, width), 1)).astype(F32)
    hits = columns == target
    local_top = jnp.max(logits, axis=1, keepdims=True)
    expo = jnp.exp(logits - local_top)
    local_total = jnp.sum(expo, axis=1, keepdims=True)
    local_picked = jnp.sum(jnp.where(hits, logits, 0.0), axis=1, keepdims=True)
    e_v[...] = expo
    lane = lax.broadcasted_iota(jnp.int32, (tokens, 128), 1)
    packed = jnp.where(lane == 0, local_top, jnp.where(lane == 1, local_total, local_picked))
    stats[me] = jnp.transpose(packed)[0:8, :]
    for k in range(1, n):
        copy = remote(stats.at[me], stats.at[me], st_send.at[k], st_recv.at[me], lax.rem(me + k, n))
        copy.start()
        sends.append(copy)
    for k in range(1, n):
        source = lax.rem(me + k, n)
        remote(stats.at[source], stats.at[source], st_send.at[k], st_recv.at[source], source).wait_recv()

    top = stats[0, 0:1, :]
    for k in range(1, n):
        top = jnp.maximum(top, stats[k, 0:1, :])
    total = jnp.zeros_like(top)
    picked = jnp.zeros_like(top)
    for k in range(n):
        total += stats[k, 1:2, :] * jnp.exp(stats[k, 0:1, :] - top)
        picked += stats[k, 2:3, :]
    loss_ref[...] = jnp.sum(top + jnp.log(total) - picked, axis=1, keepdims=True) / tokens

    sub = lax.broadcasted_iota(jnp.int32, (128, tokens), 0)
    turned = jnp.transpose(jnp.where(sub == 0, top, total))
    factor = jnp.exp(local_top - turned[:, 0:1]) / turned[:, 1:2]
    grad = (e_v[...] * factor - hits.astype(F32)).astype(BF16)
    g_ref[...] = grad

    def pair_copy(j):
        return remote(part.at[j, 1 - core], xbuf.at[j], x_send.at[j], x_recv.at[j], partner)

    def group_copy(j, k):
        return remote(outb.at[j, other(k)], rbuf.at[j, chip], rs_send.at[j, k], rs_recv.at[j, chip], other(k) * 2 + core)

    def pass_on(j):
        pair_copy(j).wait_recv()
        for z in range(chips):
            outb[j, z] = (part[j, core, z] + xbuf[j, z]).astype(BF16)
        for k in range(1, chips):
            copy = group_copy(j, k)
            copy.start()
            sends.append(copy)

    for j in range(parts):
        term = lax.dot_general(
            g_ref[...], w_v[j * wide:(j + 1) * wide, :], (((1,), (1,)), ((), ())), preferred_element_type=F32
        )
        for z in range(chips):
            for half in range(2):
                at = (2 * z + half) * rows
                part[j, half, z] = term[at:at + rows, :]
        copy = pair_copy(j)
        copy.start()
        sends.append(copy)
        if j > 0:
            pass_on(j - 1)
    pass_on(parts - 1)

    for j in range(parts):
        summed = part[j, core, chip] + xbuf[j, chip]
        for k in range(1, chips):
            source = other(k)
            remote(rbuf.at[j, source], rbuf.at[j, source], rs_send.at[j, k], rs_recv.at[j, source], source * 2 + core).wait_recv()
            summed += rbuf[j, source].astype(F32)
        dh_ref[:, j * wide:(j + 1) * wide] = summed.astype(BF16)

    for copy in sends:
        copy.wait_send()


def weight_kernel(hid_ref, g_ref, out_ref):
    out_ref[...] = lax.dot_general(
        hid_ref[...], g_ref[...], (((0,), (0,)), ((), ())), preferred_element_type=F32
    ).astype(BF16)


def body(n, hidden, weight, targets):
    rows, depth = hidden.shape
    width = weight.shape[1]
    tokens = rows * n
    chips = n // 2
    pieces = split(depth, 2, 256)
    parts = split(depth, 4, 256)
    span, wide = depth // pieces, depth // parts
    vmem = pl.BlockSpec(memory_space=pltpu.VMEM)
    dma = pltpu.SemaphoreType.DMA
    hid, grad, d_hidden, loss = pl.pallas_call(
        functools.partial(loss_kernel, n),
        out_shape=(
            jax.ShapeDtypeStruct((tokens, depth), BF16),
            jax.ShapeDtypeStruct((tokens, width), BF16),
            jax.ShapeDtypeStruct((rows, depth), BF16),
            jax.ShapeDtypeStruct((1, 1), F32),
        ),
        in_specs=[vmem, pl.BlockSpec(memory_space=pl.ANY), vmem],
        out_specs=(vmem, vmem, vmem, vmem),
        scratch_shapes=[
            pltpu.VMEM((depth, width), BF16),
            pltpu.VMEM((pieces, n, rows, span), BF16),
            pltpu.VMEM((tokens, width), F32),
            pltpu.VMEM((n, 8, tokens), F32),
            pltpu.VMEM((parts, 2, chips, rows, wide), F32),
            pltpu.VMEM((parts, chips, rows, wide), F32),
            pltpu.VMEM((parts, chips, rows, wide), BF16),
            pltpu.VMEM((parts, chips, rows, wide), BF16),
            dma((pieces,)),
            dma((pieces, chips)),
            dma((pieces, chips)),
            dma((pieces, n)),
            dma((n,)),
            dma((n,)),
            dma((parts,)),
            dma((parts,)),
            dma((parts, chips)),
            dma((parts, chips)),
        ],
        compiler_params=pltpu.CompilerParams(
            collective_id=0, has_side_effects=True, vmem_limit_bytes=50 * 1024 * 1024
        ),
    )(hidden, weight, targets.reshape(1, tokens))
    block = depth // split(depth, 6, 256)
    d_weight = pl.pallas_call(
        weight_kernel,
        grid=(depth // block,),
        out_shape=jax.ShapeDtypeStruct((depth, width), BF16),
        in_specs=[
            pl.BlockSpec((tokens, block), lambda i: (0, i)),
            pl.BlockSpec((tokens, width), lambda i: (0, 0)),
        ],
        out_specs=pl.BlockSpec((block, width), lambda i: (i, 0)),
    )(hid, grad)
    return loss.reshape(1), d_hidden, d_weight


def solution(mesh):
    placed = (P(("dp", "vocab"), None), P(None, "vocab"), P("dp"))
    return jax.shard_map(
        functools.partial(body, mesh.shape["vocab"]),
        mesh=mesh,
        in_specs=placed,
        out_specs=(P("dp"), P(("dp", "vocab"), None), P("dp", "vocab")),
        check_vma=False,
    )
```

time: 97.1 us -> 38.9 us (0.40)
  blocking collectives: 67.4 us -> 0 us
  Pallas kernels: 0 us -> 32.6 us
  matrix products: 13.5 us -> 0 us
  local copies, waits for them, and re-layouts: 11.4 us -> 3.47 us
  other arithmetic: 1.03 us -> 0 us
    psum x1 -> x0, blocking collectives: 33.8 us -> none  [body(): everything = lax.psum(partial_value, 'vocab')]
    pallas_call x0 -> x2, Pallas kernels: none -> 32.6 us  [the longest x1 26.5 us: body(): pl.pallas_call(functools.partial(loss_kernel, n), out_shape=(jax.ShapeDty...]
    unnamed x1 -> x0, blocking collectives: 17.2 us -> none
    all_gather x1 -> x0, blocking collectives: 16.4 us -> none  [body(): gathered = lax.all_gather(hidden, 'vocab', axis=0, tiled=True)]
    dot_general x3 -> x0, matrix products: 13.5 us -> none  [the longest x1 4.85 us: body(): lax.dot_general(grad_logits, weight, (((1,), (1,)), ((), ())), preferred_...]
    unnamed x10 -> x9, local copies, waits for them, and re-layouts: 10.5 us -> 3.47 us
where the time goes in v1:
time: 38.9 us; the launch traced here: 38.5 us
  Pallas kernels  32.6 us (84%)
  local copies, waits for them, and re-layouts  3.47 us (9%)
  between operations  2.46 us (6%)
    pallas_call x1, Pallas kernels, body(): pl.pallas_call(functools.partial(loss_kernel, n), out_shape=(jax.ShapeDty...  26.5 us
    pallas_call x1, Pallas kernels, body(): pl.pallas_call(weight_kernel, grid=(depth // block,), out_shape=jax.Shape...  6.13 us
    unnamed x9, local copies, waits for them, and re-layouts  3.47 us

profile of v1, /device:TPU:0, one launch (start us, length us, event | category | flops | bytes accessed | tf_op | source)
XLA Modules:
  0.0 38.5 jit_solution(3472143678119538872)
XLA Ops:
  0.6 0.0 copy-start.2
  0.6 0.8 %copy-done.2 = bf16[8,3072]{1,0:T(8,128)(2,1)S(1)} copy-done((bf16[8,3072]{1,0:T(8,128)(2,1)S(1)}, bf16[8,3072]{1,0:T(8,128)(2,1)}, u32[]{:S(2)}) %copy-start.2) | copy-done | bytes 49176
  1.4 0.0 copy-start.3
  1.4 0.7 %copy-done.3 = s32[64]{0:T(128)S(1)} copy-done((s32[64]{0:T(128)S(1)}, s32[64]{0:T(128)}, u32[]{:S(2)}) %copy-start.3) | copy-done | bytes 280
  2.1 26.5 %shard_map.58 = (bf16[64,3072]{1,0:T(8,128)(2,1)S(1)}, bf16[64,1024]{1,0:T(8,128)(2,1)S(1)}, bf16[8,3072]{1,0:T(8,128)(2,1)S(1)}, f32[1,1]{1,0:T(1,128)}) custom-call(bf16[8,3072]{1,0:T(8,128)(2,1)S(1)} %copy-done.2, bf16[3072,1024]{1,0:T(8,128)(2,1)} %w_hbm.1, s32[1,64]{1,0:T(1,128)S(1)} %bitcast.2), custom_call_target="tpu_custom_call" | custom-call | tf_op jit(solution)/shard_map/pallas_call | solution.py:184
  28.6 0.0 copy-start
  28.6 0.7 %copy-done = bf16[64,3072]{1,0:T(8,128)(2,1)} copy-done((bf16[64,3072]{1,0:T(8,128)(2,1)}, bf16[64,3072]{1,0:T(8,128)(2,1)S(1)}, u32[]{:S(2)}) %copy-start) | copy-done | bytes 393240
  29.3 0.0 copy-start.1
  29.3 0.7 %copy-done.1 = bf16[64,1024]{1,0:T(8,128)(2,1)} copy-done((bf16[64,1024]{1,0:T(8,128)(2,1)}, bf16[64,1024]{1,0:T(8,128)(2,1)S(1)}, u32[]{:S(2)}) %copy-start.1) | copy-done | bytes 131096
  30.0 6.1 %shard_map.59 = bf16[3072,1024]{1,0:T(8,128)(2,1)} custom-call(bf16[64,3072]{1,0:T(8,128)(2,1)} %copy-done, bf16[64,1024]{1,0:T(8,128)(2,1)} %copy-done.1), custom_call_target="tpu_custom_call" | custom-call | tf_op jit(solution)/shard_map/pallas_call | solution.py:219
  36.8 0.6 %copy.9 = bf16[8,3072]{1,0:T(8,128)(2,1)} copy(bf16[8,3072]{1,0:T(8,128)(2,1)S(1)} %get-tuple-element.15) | data formatting | bytes 98304
Async XLA Ops:
  0.6 0.8 %copy-start.2 = (bf16[8,3072]{1,0:T(8,128)(2,1)S(1)}, bf16[8,3072]{1,0:T(8,128)(2,1)}, u32[]{:S(2)}) copy-start(bf16[8,3072]{1,0:T(8,128)(2,1)} %h_ref.1) | copy-start | bytes 147460
  1.4 0.7 %copy-start.3 = (s32[64]{0:T(128)S(1)}, s32[64]{0:T(128)}, u32[]{:S(2)}) copy-start(s32[64]{0:T(128)} %param.5) | copy-start | bytes 772
  28.6 0.7 %copy-start = (bf16[64,3072]{1,0:T(8,128)(2,1)}, bf16[64,3072]{1,0:T(8,128)(2,1)S(1)}, u32[]{:S(2)}) copy-start(bf16[64,3072]{1,0:T(8,128)(2,1)S(1)} %get-tuple-element.9.hid_ref) | copy-start | bytes 1179652
  29.3 0.7 %copy-start.1 = (bf16[64,1024]{1,0:T(8,128)(2,1)}, bf16[64,1024]{1,0:T(8,128)(2,1)S(1)}, u32[]{:S(2)}) copy-start(bf16[64,1024]{1,0:T(8,128)(2,1)S(1)} %get-tuple-element.10.g_ref) | copy-start | bytes 393220

commit v2 on v1

--- a/solution.py
+++ b/solution.py
@@ -26,9 +26,9 @@
 
 
 def loss_kernel(
-    n, h_ref, w_hbm, t_ref, hid_ref, g_ref, dh_ref, loss_ref,
-    w_v, slots, e_v, stats, part, xbuf, outb, rbuf,
-    w_sem, ag_send, fw_send, ag_recv, st_send, st_recv, x_send, x_recv, rs_send, rs_recv,
+    n, h_hbm, w_hbm, t_hbm, dw_ref, dh_ref, loss_ref,
+    h_ref, t_ref, hid_ref, turned_ref, g_ref, w_v, slots, e_v, stats, part, xbuf, outb, rbuf,
+    in_sem, w_sem, ag_send, fw_send, ag_recv, st_send, st_recv, x_send, x_recv, rs_send, rs_recv,
 ):
     me = lax.axis_index("vocab")
     chips = n // 2
@@ -38,10 +38,18 @@
     tokens, width = e_v.shape
     pieces, span = slots.shape[0], slots.shape[3]
     parts, wide = part.shape[0], part.shape[4]
+    blocks = split(depth, 6, 256)
+    tall = depth // blocks
+
+    above = chips - 1 - chip
 
     def other(k):
-        return lax.rem(chip + k, chips)
-
+        up = (above - k + chips) // chips
+        return up * (chips - k) + (1 - up) * (k - 1 - above)
+
+    takes = [pltpu.make_async_copy(h_hbm, h_ref, in_sem.at[0]), pltpu.make_async_copy(t_hbm, t_ref, in_sem.at[1])]
+    for take in takes:
+        take.start()
     loads = [
         pltpu.make_async_copy(w_hbm.at[pl.ds(a * span, span), :], w_v.at[pl.ds(a * span, span), :], w_sem.at[a])
         for a in range(pieces)
@@ -52,6 +60,8 @@
     barrier = pltpu.get_barrier_semaphore()
     for k in range(1, n):
         pl.semaphore_signal(barrier, inc=1, device_id={"vocab": lax.rem(me + k, n)}, device_id_type=MESH)
+    for take in takes:
+        take.wait()
     for a in range(pieces):
         slots[a, me] = h_ref[:, a * span:(a + 1) * span]
     pl.semaphore_wait(barrier, n - 1)
@@ -66,14 +76,14 @@
             sends.append(copy)
 
     for a in range(pieces):
-        for k in range(1, chips):
+        for k in range(chips - 1, 0, -1):
             source = other(k) * 2 + core
             copy = remote(slots.at[a, source], slots.at[a, source], fw_send.at[a, k], ag_recv.at[a, source], partner)
             copy.wait_recv()
             copy.start()
             sends.append(copy)
         for k in range(chips):
-            source = other(k) * 2 + (1 - core)
+            source = partner if k == 0 else other(k) * 2 + (1 - core)
             remote(slots.at[a, source], slots.at[a, source], fw_send.at[a, k], ag_recv.at[a, source], partner).wait_recv()
         for z in range(chips):
             both = jnp.concatenate([slots[a, 2 * z].astype(F32), slots[a, 2 * z + 1].astype(F32)], axis=0)
@@ -103,6 +113,8 @@
         copy = remote(stats.at[me], stats.at[me], st_send.at[k], st_recv.at[me], lax.rem(me + k, n))
         copy.start()
         sends.append(copy)
+    for b in range(blocks):
+        turned_ref[b * tall:(b + 1) * tall, :] = jnp.transpose(hid_ref[:, b * tall:(b + 1) * tall])
     for k in range(1, n):
         source = lax.rem(me + k, n)
         remote(stats.at[source], stats.at[source], st_send.at[k], st_recv.at[source], source).wait_recv()
@@ -152,6 +164,10 @@
         if j > 0:
             pass_on(j - 1)
     pass_on(parts - 1)
+    for b in range(blocks):
+        dw_ref[b * tall:(b + 1) * tall, :] = jnp.dot(
+            turned_ref[b * tall:(b + 1) * tall, :], g_ref[...], preferred_element_type=F32
+        ).astype(BF16)
 
     for j in range(parts):
         summed = part[j, core, chip] + xbuf[j, chip]
@@ -165,10 +181,17 @@
         copy.wait_send()
 
 
-def weight_kernel(hid_ref, g_ref, out_ref):
-    out_ref[...] = lax.dot_general(
-        hid_ref[...], g_ref[...], (((0,), (0,)), ((), ())), preferred_element_type=F32
-    ).astype(BF16)
+def store_kernel(dw_v, dh_v, loss_v, dw_hbm, dh_hbm, loss_hbm, sem):
+    copies = [pltpu.make_async_copy(dh_v, dh_hbm, sem.at[0]), pltpu.make_async_copy(loss_v, loss_hbm, sem.at[1])]
+    count = sem.shape[0] - 2
+    tall = dw_v.shape[0] // count
+    for b in range(count):
+        at = pl.ds(b * tall, tall)
+        copies.append(pltpu.make_async_copy(dw_v.at[at, :], dw_hbm.at[at, :], sem.at[2 + b]))
+    for copy in copies:
+        copy.start()
+    for copy in copies:
+        copy.wait()
 
 
 def body(n, hidden, weight, targets):
@@ -181,17 +204,23 @@
     span, wide = depth // pieces, depth // parts
     vmem = pl.BlockSpec(memory_space=pltpu.VMEM)
     dma = pltpu.SemaphoreType.DMA
-    hid, grad, d_hidden, loss = pl.pallas_call(
+    hbm = pl.BlockSpec(memory_space=pltpu.HBM)
+    results = (
+        jax.ShapeDtypeStruct((depth, width), BF16),
+        jax.ShapeDtypeStruct((rows, depth), BF16),
+        jax.ShapeDtypeStruct((1, 1), F32),
+    )
+    held = pl.pallas_call(
         functools.partial(loss_kernel, n),
-        out_shape=(
-            jax.ShapeDtypeStruct((tokens, depth), BF16),
-            jax.ShapeDtypeStruct((tokens, width), BF16),
-            jax.ShapeDtypeStruct((rows, depth), BF16),
-            jax.ShapeDtypeStruct((1, 1), F32),
-        ),
-        in_specs=[vmem, pl.BlockSpec(memory_space=pl.ANY), vmem],
-        out_specs=(vmem, vmem, vmem, vmem),
+        out_shape=results,
+        in_specs=[hbm, hbm, hbm],
+        out_specs=(vmem, vmem, vmem),
         scratch_shapes=[
+            pltpu.VMEM((rows, depth), BF16),
+            pltpu.VMEM((1, tokens), jnp.int32),
+            pltpu.VMEM((tokens, depth), BF16),
+            pltpu.VMEM((depth, tokens), BF16),
+            pltpu.VMEM((tokens, width), BF16),
             pltpu.VMEM((depth, width), BF16),
             pltpu.VMEM((pieces, n, rows, span), BF16),
             pltpu.VMEM((tokens, width), F32),
@@ -200,6 +229,7 @@
             pltpu.VMEM((parts, chips, rows, wide), F32),
             pltpu.VMEM((parts, chips, rows, wide), BF16),
             pltpu.VMEM((parts, chips, rows, wide), BF16),
+            dma((2,)),
             dma((pieces,)),
             dma((pieces, chips)),
             dma((pieces, chips)),
@@ -212,20 +242,17 @@
             dma((parts, chips)),
         ],
         compiler_params=pltpu.CompilerParams(
-            collective_id=0, has_side_effects=True, vmem_limit_bytes=50 * 1024 * 1024
+            collective_id=0, has_side_effects=True, vmem_limit_bytes=44 * 1024 * 1024
         ),
     )(hidden, weight, targets.reshape(1, tokens))
-    block = depth // split(depth, 6, 256)
-    d_weight = pl.pallas_call(
-        weight_kernel,
-        grid=(depth // block,),
-        out_shape=jax.ShapeDtypeStruct((depth, width), BF16),
-        in_specs=[
-            pl.BlockSpec((tokens, block), lambda i: (0, i)),
-            pl.BlockSpec((tokens, width), lambda i: (0, 0)),
-        ],
-        out_specs=pl.BlockSpec((block, width), lambda i: (i, 0)),
-    )(hid, grad)
+    d_weight, d_hidden, loss = pl.pallas_call(
+        store_kernel,
+        out_shape=results,
+        in_specs=[vmem, vmem, vmem],
+        out_specs=(hbm, hbm, hbm),
+        scratch_shapes=[dma((6,))],
+        compiler_params=pltpu.CompilerParams(vmem_limit_bytes=2 * 1024 * 1024),
+    )(*held)
     return loss.reshape(1), d_hidden, d_weight
 
 

time: 38.9 us -> 31.5 us (0.81)
  Pallas kernels: 32.6 us -> 29.2 us
  local copies, waits for them, and re-layouts: 3.47 us -> 1.45 us
  between operations: 2.46 us -> 0.65 us
    pallas_call x2, Pallas kernels: 32.6 us -> 29.2 us  [the longest x1 25.8 us: body(): pl.pallas_call(functools.partial(loss_kernel, n), out_shape=results, in_s...]
    unnamed x9 -> x4, local copies, waits for them, and re-layouts: 3.47 us -> 1.45 us
where the time goes in v2:
time: 31.5 us; the launch traced here: 31.3 us
  Pallas kernels  29.2 us (93%)
  local copies, waits for them, and re-layouts  1.45 us (5%)
  between operations  0.65 us (2%)
    pallas_call x1, Pallas kernels, body(): pl.pallas_call(functools.partial(loss_kernel, n), out_shape=results, in_s...  25.8 us
    pallas_call x1, Pallas kernels, body(): pl.pallas_call(store_kernel, out_shape=results, in_specs=[vmem, vmem, vme...  3.37 us
    unnamed x4, local copies, waits for them, and re-layouts  1.45 us

profile of v2, /device:TPU:0, one launch (start us, length us, event | category | flops | bytes accessed | tf_op | source)
XLA Modules:
  0.0 31.3 jit_solution(2489250118876314484)
XLA Ops:
  0.6 0.0 copy-start
  0.6 0.8 %copy-done = bf16[8,3072]{1,0:T(8,128)(2,1)S(1)} copy-done((bf16[8,3072]{1,0:T(8,128)(2,1)S(1)}, bf16[8,3072]{1,0:T(8,128)(2,1)}, u32[]{:S(2)}) %copy-start) | copy-done | bytes 49176
  1.4 0.0 copy-start.1
  1.4 0.7 %copy-done.1 = s32[64]{0:T(128)S(1)} copy-done((s32[64]{0:T(128)S(1)}, s32[64]{0:T(128)}, u32[]{:S(2)}) %copy-start.1) | copy-done | bytes 280
  2.1 25.8 %shard_map.58 = (bf16[3072,1024]{1,0:T(8,128)(2,1)S(1)}, bf16[8,3072]{1,0:T(8,128)(2,1)S(1)}, f32[1,1]{1,0:T(1,128)}) custom-call(bf16[8,3072]{1,0:T(8,128)(2,1)S(1)} %copy-done, bf16[3072,1024]{1,0:T(8,128)(2,1)} %w_hbm.1, s32[1,64]{1,0:T(1,128)S(1)} %bitcast.2), custom_call_target="tpu_custom_call" | custom-call | tf_op jit(solution)/shard_map/pallas_call | solution.py:213
  27.9 3.4 %shard_map.59 = (bf16[3072,1024]{1,0:T(8,128)(2,1)}, bf16[8,3072]{1,0:T(8,128)(2,1)}, f32[1,1]{1,0:T(1,128)}) custom-call(bf16[3072,1024]{1,0:T(8,128)(2,1)S(1)} %get-tuple-element.9.dw_v, bf16[8,3072]{1,0:T(8,128)(2,1)S(1)} %get-tuple-element.10.dh_v, f32[1,1]{1,0:T(1,128)} %get-tuple-element.11.loss_v), custom_call_target="tpu_custom_call" | custom-call | tf_op jit(solution)/shard_map/pallas_call | solution.py:248
Async XLA Ops:
  0.6 0.8 %copy-start = (bf16[8,3072]{1,0:T(8,128)(2,1)S(1)}, bf16[8,3072]{1,0:T(8,128)(2,1)}, u32[]{:S(2)}) copy-start(bf16[8,3072]{1,0:T(8,128)(2,1)} %h_hbm.1) | copy-start | bytes 147460
  1.4 0.7 %copy-start.1 = (s32[64]{0:T(128)S(1)}, s32[64]{0:T(128)}, u32[]{:S(2)}) copy-start(s32[64]{0:T(128)} %param.5) | copy-start | bytes 772

commit v3 on v2

--- a/solution.py
+++ b/solution.py
@@ -127,7 +127,7 @@
     for k in range(n):
         total += stats[k, 1:2, :] * jnp.exp(stats[k, 0:1, :] - top)
         picked += stats[k, 2:3, :]
-    loss_ref[...] = jnp.sum(top + jnp.log(total) - picked, axis=1, keepdims=True) / tokens
+    loss_ref[...] = jnp.broadcast_to(jnp.sum(top + jnp.log(total) - picked, axis=1, keepdims=True) / tokens, loss_ref.shape)
 
     sub = lax.broadcasted_iota(jnp.int32, (128, tokens), 0)
     turned = jnp.transpose(jnp.where(sub == 0, top, total))
@@ -181,13 +181,16 @@
         copy.wait_send()
 
 
-def store_kernel(dw_v, dh_v, loss_v, dw_hbm, dh_hbm, loss_hbm, sem):
-    copies = [pltpu.make_async_copy(dh_v, dh_hbm, sem.at[0]), pltpu.make_async_copy(loss_v, loss_hbm, sem.at[1])]
+def store_kernel(dw_v, dh_v, loss_v, dw_hbm, dh_hbm, loss_hbm, one_v, sem):
+    one_v[...] = loss_v[0:1, 0:1]
+    copies = []
     count = sem.shape[0] - 2
     tall = dw_v.shape[0] // count
     for b in range(count):
         at = pl.ds(b * tall, tall)
         copies.append(pltpu.make_async_copy(dw_v.at[at, :], dw_hbm.at[at, :], sem.at[2 + b]))
+    copies.append(pltpu.make_async_copy(dh_v, dh_hbm, sem.at[0]))
+    copies.append(pltpu.make_async_copy(one_v, loss_hbm, sem.at[1]))
     for copy in copies:
         copy.start()
     for copy in copies:
@@ -199,20 +202,17 @@
     width = weight.shape[1]
     tokens = rows * n
     chips = n // 2
-    pieces = split(depth, 2, 256)
+    pieces = split(depth, 4, 256)
     parts = split(depth, 4, 256)
     span, wide = depth // pieces, depth // parts
     vmem = pl.BlockSpec(memory_space=pltpu.VMEM)
     dma = pltpu.SemaphoreType.DMA
     hbm = pl.BlockSpec(memory_space=pltpu.HBM)
-    results = (
-        jax.ShapeDtypeStruct((depth, width), BF16),
-        jax.ShapeDtypeStruct((rows, depth), BF16),
-        jax.ShapeDtypeStruct((1, 1), F32),
-    )
+    shared = (jax.ShapeDtypeStruct((depth, width), BF16), jax.ShapeDtypeStruct((rows, depth), BF16))
+    tile = jax.ShapeDtypeStruct((8, 128), F32)
     held = pl.pallas_call(
         functools.partial(loss_kernel, n),
-        out_shape=results,
+        out_shape=(*shared, tile),
         in_specs=[hbm, hbm, hbm],
         out_specs=(vmem, vmem, vmem),
         scratch_shapes=[
@@ -242,15 +242,15 @@
             dma((parts, chips)),
         ],
         compiler_params=pltpu.CompilerParams(
-            collective_id=0, has_side_effects=True, vmem_limit_bytes=44 * 1024 * 1024
+            collective_id=0, has_side_effects=True, vmem_limit_bytes=45 * 1024 * 1024
         ),
     )(hidden, weight, targets.reshape(1, tokens))
     d_weight, d_hidden, loss = pl.pallas_call(
         store_kernel,
-        out_shape=results,
+        out_shape=(*shared, jax.ShapeDtypeStruct((1, 1), F32)),
         in_specs=[vmem, vmem, vmem],
         out_specs=(hbm, hbm, hbm),
-        scratch_shapes=[dma((6,))],
+        scratch_shapes=[pltpu.VMEM((1, 1), F32), dma((2 + split(depth, 12, 16),))],
         compiler_params=pltpu.CompilerParams(vmem_limit_bytes=2 * 1024 * 1024),
     )(*held)
     return loss.reshape(1), d_hidden, d_weight

time: 31.5 us -> 31.9 us (1.013)
  Pallas kernels: 29.2 us -> 29.6 us
    pallas_call x2, Pallas kernels: 29.2 us -> 29.6 us  [the longest x1 26.8 us: body(): pl.pallas_call(functools.partial(loss_kernel, n), out_shape=(*shared, til...]
where the time goes in v3:
time: 31.9 us; the launch traced here: 31.7 us
  Pallas kernels  29.6 us (93%)
  local copies, waits for them, and re-layouts  1.45 us (5%)
  between operations  0.65 us (2%)
    pallas_call x1, Pallas kernels, body(): pl.pallas_call(functools.partial(loss_kernel, n), out_shape=(*shared, til...  26.8 us
    pallas_call x1, Pallas kernels, body(): pl.pallas_call(store_kernel, out_shape=(*shared, jax.ShapeDtypeStruct((1,...  2.77 us
    unnamed x4, local copies, waits for them, and re-layouts  1.45 us

profile of v3, /device:TPU:0, one launch (start us, length us, event | category | flops | bytes accessed | tf_op | source)
XLA Modules:
  0.0 31.7 jit_solution(8790247697946385228)
XLA Ops:
  0.6 0.0 copy-start
  0.6 0.8 %copy-done = bf16[8,3072]{1,0:T(8,128)(2,1)S(1)} copy-done((bf16[8,3072]{1,0:T(8,128)(2,1)S(1)}, bf16[8,3072]{1,0:T(8,128)(2,1)}, u32[]{:S(2)}) %copy-start) | copy-done | bytes 49176
  1.4 0.0 copy-start.1
  1.4 0.7 %copy-done.1 = s32[64]{0:T(128)S(1)} copy-done((s32[64]{0:T(128)S(1)}, s32[64]{0:T(128)}, u32[]{:S(2)}) %copy-start.1) | copy-done | bytes 280
  2.1 26.8 %shard_map.58 = (bf16[3072,1024]{1,0:T(8,128)(2,1)S(1)}, bf16[8,3072]{1,0:T(8,128)(2,1)S(1)}, f32[8,128]{1,0:T(8,128)S(1)}) custom-call(bf16[8,3072]{1,0:T(8,128)(2,1)S(1)} %copy-done, bf16[3072,1024]{1,0:T(8,128)(2,1)} %w_hbm.1, s32[1,64]{1,0:T(1,128)S(1)} %bitcast.2), custom_call_target="tpu_custom_call" | custom-call | tf_op jit(solution)/shard_map/pallas_call | solution.py:213
  28.9 2.8 %shard_map.59 = (bf16[3072,1024]{1,0:T(8,128)(2,1)}, bf16[8,3072]{1,0:T(8,128)(2,1)}, f32[1,1]{1,0:T(1,128)}) custom-call(bf16[3072,1024]{1,0:T(8,128)(2,1)S(1)} %get-tuple-element.9.dw_v, bf16[8,3072]{1,0:T(8,128)(2,1)S(1)} %get-tuple-element.10.dh_v, f32[8,128]{1,0:T(8,128)S(1)} %get-tuple-element.11.loss_v), custom_call_target="tpu_custom_call" | custom-call | tf_op jit(solution)/shard_map/pallas_call | solution.py:248
Async XLA Ops:
  0.6 0.8 %copy-start = (bf16[8,3072]{1,0:T(8,128)(2,1)S(1)}, bf16[8,3072]{1,0:T(8,128)(2,1)}, u32[]{:S(2)}) copy-start(bf16[8,3072]{1,0:T(8,128)(2,1)} %h_hbm.1) | copy-start | bytes 147460
  1.4 0.7 %copy-start.1 = (s32[64]{0:T(128)S(1)}, s32[64]{0:T(128)}, u32[]{:S(2)}) copy-start(s32[64]{0:T(128)} %param.5) | copy-start | bytes 772

commit v4 on v3

--- a/solution.py
+++ b/solution.py
@@ -27,7 +27,7 @@
 
 def loss_kernel(
     n, h_hbm, w_hbm, t_hbm, dw_ref, dh_ref, loss_ref,
-    h_ref, t_ref, hid_ref, turned_ref, g_ref, w_v, slots, e_v, stats, part, xbuf, outb, rbuf,
+    h_ref, t_ref, aim_ref, hid_ref, turned_ref, g_ref, w_v, slots, e_v, stats, part, xbuf, outb, rbuf,
     in_sem, w_sem, ag_send, fw_send, ag_recv, st_send, st_recv, x_send, x_recv, rs_send, rs_recv,
 ):
     me = lax.axis_index("vocab")
@@ -64,6 +64,7 @@
         take.wait()
     for a in range(pieces):
         slots[a, me] = h_ref[:, a * span:(a + 1) * span]
+    aim_ref[...] = jnp.transpose(jnp.broadcast_to((t_ref[...] - me * width).astype(F32), (128, tokens)))
     pl.semaphore_wait(barrier, n - 1)
 
     sends = []
@@ -98,9 +99,7 @@
             e_v[...] += term
 
     logits = e_v[...]
-    target = jnp.transpose(jnp.broadcast_to(t_ref[...].astype(F32), (128, tokens)))[:, 0:1]
-    columns = (me * width + lax.broadcasted_iota(jnp.int32, (tokens, width), 1)).astype(F32)
-    hits = columns == target
+    hits = lax.broadcasted_iota(jnp.int32, (tokens, width), 1).astype(F32) == aim_ref[:, 0:1]
     local_top = jnp.max(logits, axis=1, keepdims=True)
     expo = jnp.exp(logits - local_top)
     local_total = jnp.sum(expo, axis=1, keepdims=True)
@@ -202,8 +201,8 @@
     width = weight.shape[1]
     tokens = rows * n
     chips = n // 2
-    pieces = split(depth, 4, 256)
-    parts = split(depth, 4, 256)
+    pieces = split(depth, 2, 256)
+    parts = split(depth, 6, 256)
     span, wide = depth // pieces, depth // parts
     vmem = pl.BlockSpec(memory_space=pltpu.VMEM)
     dma = pltpu.SemaphoreType.DMA
@@ -218,6 +217,7 @@
         scratch_shapes=[
             pltpu.VMEM((rows, depth), BF16),
             pltpu.VMEM((1, tokens), jnp.int32),
+            pltpu.VMEM((tokens, 128), F32),
             pltpu.VMEM((tokens, depth), BF16),
             pltpu.VMEM((depth, tokens), BF16),
             pltpu.VMEM((tokens, width), BF16),

time: 31.9 us -> 30.8 us (0.966)
  Pallas kernels: 29.6 us -> 28.5 us
    pallas_call x1, Pallas kernels: 26.8 us -> 25.7 us  [body(): pl.pallas_call(functools.partial(loss_kernel, n), out_shape=(*shared, til...]
where the time goes in v4:
time: 30.8 us; the launch traced here: 30.6 us
  Pallas kernels  28.5 us (93%)
  local copies, waits for them, and re-layouts  1.45 us (5%)
  between operations  0.65 us (2%)
    pallas_call x1, Pallas kernels, body(): pl.pallas_call(functools.partial(loss_kernel, n), out_shape=(*shared, til...  25.7 us
    pallas_call x1, Pallas kernels, body(): pl.pallas_call(store_kernel, out_shape=(*shared, jax.ShapeDtypeStruct((1,...  2.77 us
    unnamed x4, local copies, waits for them, and re-layouts  1.45 us

profile of v4, /device:TPU:0, one launch (start us, length us, event | category | flops | bytes accessed | tf_op | source)
XLA Modules:
  0.0 30.6 jit_solution(15074724574860486947)
XLA Ops:
  0.6 0.0 copy-start
  0.6 0.8 %copy-done = bf16[8,3072]{1,0:T(8,128)(2,1)S(1)} copy-done((bf16[8,3072]{1,0:T(8,128)(2,1)S(1)}, bf16[8,3072]{1,0:T(8,128)(2,1)}, u32[]{:S(2)}) %copy-start) | copy-done | bytes 49176
  1.4 0.0 copy-start.1
  1.4 0.7 %copy-done.1 = s32[64]{0:T(128)S(1)} copy-done((s32[64]{0:T(128)S(1)}, s32[64]{0:T(128)}, u32[]{:S(2)}) %copy-start.1) | copy-done | bytes 280
  2.1 25.7 %shard_map.58 = (bf16[3072,1024]{1,0:T(8,128)(2,1)S(1)}, bf16[8,3072]{1,0:T(8,128)(2,1)S(1)}, f32[8,128]{1,0:T(8,128)S(1)}) custom-call(bf16[8,3072]{1,0:T(8,128)(2,1)S(1)} %copy-done, bf16[3072,1024]{1,0:T(8,128)(2,1)} %w_hbm.1, s32[1,64]{1,0:T(1,128)S(1)} %bitcast.2), custom_call_target="tpu_custom_call" | custom-call | tf_op jit(solution)/shard_map/pallas_call | solution.py:212
  27.8 2.8 %shard_map.59 = (bf16[3072,1024]{1,0:T(8,128)(2,1)}, bf16[8,3072]{1,0:T(8,128)(2,1)}, f32[1,1]{1,0:T(1,128)}) custom-call(bf16[3072,1024]{1,0:T(8,128)(2,1)S(1)} %get-tuple-element.9.dw_v, bf16[8,3072]{1,0:T(8,128)(2,1)S(1)} %get-tuple-element.10.dh_v, f32[8,128]{1,0:T(8,128)S(1)} %get-tuple-element.11.loss_v), custom_call_target="tpu_custom_call" | custom-call | tf_op jit(solution)/shard_map/pallas_call | solution.py:248
Async XLA Ops:
  0.6 0.8 %copy-start = (bf16[8,3072]{1,0:T(8,128)(2,1)S(1)}, bf16[8,3072]{1,0:T(8,128)(2,1)}, u32[]{:S(2)}) copy-start(bf16[8,3072]{1,0:T(8,128)(2,1)} %h_hbm.1) | copy-start | bytes 147460
  1.4 0.7 %copy-start.1 = (s32[64]{0:T(128)S(1)}, s32[64]{0:T(128)}, u32[]{:S(2)}) copy-start(s32[64]{0:T(128)} %param.5) | copy-start | bytes 772
